TPU v7x, 32 devices: a whole 2x2x4 slice. The times are simulated.
32 devices in a mesh: grp: 2 (over x), row: 8 (over z, core), col: 2 (over y).
Axes of the slice: x: 2, y: 2, z: 4, core: 2. Of those that a mesh axis runs over, the one named last changes fastest.
Arguments:
- vectors: float32 [64, 128, 512], P('grp', 'row', 'col'), may hold values from -6 to 6
- disorder: float32 [128, 512], P('row', 'col'), may hold values from -1.5 to 1.5
Outputs:
- cheb_prev: float32 [64, 128, 512], P('grp', 'row', 'col')
- cheb_last: float32 [64, 128, 512], P('grp', 'row', 'col')
- moments: float32 [17], replicated
All inputs are finite; a program needn't handle non-finite values.
Results may differ from a plain program's by a relative error of at most 0.0001.
Values sent between devices are 32-bit elements; how exact they have to be, the bound alone decides.
No kernel may reach another device: no remote copies, remote signals or barrier semaphores. Data moves between devices by JAX's collectives and lax.ppermute only.
A program may use at most 64 MiB of HBM per device.

v0:
```python
import jax
import jax.numpy as jnp
from jax import lax
from jax.sharding import PartitionSpec as P

STEPS = 8
SCALE = 4.6


def extended(block, sides, width):
    for axis, dim in sides:
        count = lax.axis_size(axis)
        forward = [(i, i + 1) for i in range(count - 1)]
        forward.append((count - 1, 0))
        backward = [(target, source) for source, target in forward]
        low = lax.ppermute(
            lax.slice_in_dim(block, block.shape[dim] - width, None, axis=dim), axis, forward
        )
        high = lax.ppermute(lax.slice_in_dim(block, 0, width, axis=dim), axis, backward)
        block = jnp.concatenate([low, block, high], axis=dim)
    return block


def inner_hop(field, dis_part, even_part):
    left = field[:, 1:-1, :-2]
    right = field[:, 1:-1, 2:]
    below = field[:, 2:, 1:-1]
    above = field[:, :-2, 1:-1]
    center = field[:, 1:-1, 1:-1]
    vertical = jnp.where(even_part, below, above)
    return (dis_part * center - (left + right + vertical)) / SCALE


def body(vectors, disorder):
    vecs, rows_here, cols_here = vectors.shape
    count = float(
        vecs
        * lax.axis_size("grp")
        * rows_here
        * lax.axis_size("row")
        * cols_here
        * lax.axis_size("col")
    )
    margin = 4
    dis_pad = extended(disorder, (("row", 0), ("col", 1)), margin)
    rows = lax.broadcasted_iota(jnp.int32, dis_pad.shape, 0)
    cols = lax.broadcasted_iota(jnp.int32, dis_pad.shape, 1)
    even_pad = (rows + cols) % 2 == 0

    def advance(field):
        extra = (field.shape[1] - rows_here) // 2
        start = margin - extra
        stop_r = start + field.shape[1] - 1
        stop_c = start + field.shape[2] - 1
        dis_part = dis_pad[start + 1 : stop_r, start + 1 : stop_c]
        even_part = even_pad[start + 1 : stop_r, start + 1 : stop_c][None]
        return inner_hop(field, dis_part, even_part)

    def interior(field):
        extra = (field.shape[1] - rows_here) // 2
        return field[:, extra : extra + rows_here, extra : extra + cols_here]

    older = vectors
    newer = vectors
    squares = [jnp.sum(vectors * vectors)]
    crosses = []
    for rounds in range(STEPS // margin):
        padded_old, padded_new = (
            extended(older, (("row", 1), ("col", 2)), margin),
            extended(newer, (("row", 1), ("col", 2)), margin),
        )
        for inner in range(margin):
            if rounds == 0 and inner == 0:
                latest = advance(padded_new)
            else:
                latest = 2.0 * advance(padded_new) - padded_old[:, 1:-1, 1:-1]
            padded_old = padded_new[:, 1:-1, 1:-1]
            padded_new = latest
            kept_new = interior(padded_new)
            kept_old = interior(padded_old)
            squares.append(jnp.sum(kept_new * kept_new))
            crosses.append(jnp.sum(kept_new * kept_old))
        older, newer = (padded_old, padded_new)
    total_squares = [lax.psum(squares[0], ("grp", "row", "col"))]
    total_crosses = []
    for index in range(STEPS):
        pair = lax.psum((squares[index + 1], crosses[index]), ("grp", "row", "col"))
        total_squares.append(pair[0])
        total_crosses.append(pair[1])
    total_squares = jnp.stack(total_squares)
    total_crosses = jnp.stack(total_crosses)
    total_squares = total_squares / count
    total_crosses = total_crosses / count
    first = total_squares[0]
    second = total_crosses[0]
    values = [first, second]
    for index in range(1, STEPS + 1):
        values.append(2.0 * total_squares[index] - first)
        if index < STEPS:
            values.append(2.0 * total_crosses[index] - second)
    return (older, newer, jnp.stack(values))


def solution(mesh):
    placed = (P("grp", "row", "col"), P("row", "col"))
    return jax.shard_map(
        body,
        mesh=mesh,
        in_specs=placed,
        out_specs=(P("grp", "row", "col"), P("grp", "row", "col"), P()),
        check_vma=False,
    )
```

profile of v0, /device:TPU:0, one launch (start us, length us, event | category | flops | bytes accessed | tf_op | source)
XLA Modules:
  0.0 162.1 jit_solution(18027950216888657291)
XLA Ops:
  1.8 4.0 %collective-permute-start.1 = (f32[4,256]{1,0:T(4,128)S(1)}, f32[4,256]{1,0:T(4,128)S(1)}, u32[]{:S(2)}, u32[]{:S(2)}) collective-permute-start(f32[4,256]{1,0:T(4,128)S(1)} %get-tuple-element.64), channel_id=1, source_target_pairs={{2,0},{4,2},{6,4},{8,6},{10,8},{12,10},{14,12},{0,14},{3,1},{5,3},... | collective-permute-start | bytes 12296 | tf_op jit(solution)/shard_map/ppermute | solution.py:19
  5.9 1.1 fusion.39
  7.0 3.5 %collective-permute-start.5 = (f32[32,4,256]{2,1,0:T(4,128)S(1)}, f32[32,4,256]{2,1,0:T(4,128)S(1)}, u32[]{:S(2)}, u32[]{:S(2)}) collective-permute-start(f32[32,4,256]{2,1,0:T(4,128)S(1)} %get-tuple-element.60), channel_id=1, source_target_pairs={{2,0},{4,2},{6,4},{8,6},{10,8},{12,10},{14,12},{0,14},{3,1},{5,3},... | collective-permute-start | bytes 393224 | tf_op jit(solution)/shard_map/ppermute | solution.py:19
  10.9 0.7 pad_maximum_fusion.10
  11.7 2.0 %collective-permute-start.2 = (f32[24,4]{1,0:T(8,128)S(1)}, f32[24,4]{1,0:T(8,128)S(1)}, u32[]{:S(2)}, u32[]{:S(2)}) collective-permute-start(f32[24,4]{1,0:T(8,128)S(1)} %get-tuple-element.61), channel_id=1, source_target_pairs={{0,1},{1,0},{2,3},{3,2},{4,5},{5,4},{6,7},{7,6},{8,9},{9,8},{10,11... | collective-permute-start | bytes 1160 | tf_op jit(solution)/shard_map/ppermute | solution.py:16
  13.8 1.2 pad_maximum_fusion.6
  15.2 2.6 %collective-permute-start.6 = (f32[32,24,4]{2,1,0:T(8,128)S(1)}, f32[32,24,4]{2,1,0:T(8,128)S(1)}, u32[]{:S(2)}, u32[]{:S(2)}) collective-permute-start(f32[32,24,4]{2,1,0:T(8,128)S(1)} %get-tuple-element.55), channel_id=1, source_target_pairs={{0,1},{1,0},{2,3},{3,2},{4,5},{5,4},{6,7},{7,6},{8,9},{9,8},{10,11... | collective-permute-start | bytes 36872 | tf_op jit(solution)/shard_map/ppermute | solution.py:16
  18.2 9.5 %collective-permute-done.6 = f32[32,24,4]{2,1,0:T(8,128)S(1)} collective-permute-done((f32[32,24,4]{2,1,0:T(8,128)S(1)}, f32[32,24,4]{2,1,0:T(8,128)S(1)}, u32[]{:S(2)}, u32[]{:S(2)}) %collective-permute-start.6) | collective-permute-done | bytes 12320 | tf_op jit(solution)/shard_map/ppermute | solution.py:16
  27.7 6.4 %collective-permute-done.7 = f32[32,24,4]{2,1,0:T(8,128)S(1)} collective-permute-done((f32[32,24,4]{2,1,0:T(8,128)S(1)}, f32[32,24,4]{2,1,0:T(8,128)S(1)}, u32[]{:S(2)}, u32[]{:S(2)}) %collective-permute-start.7) | collective-permute-done | bytes 12320 | tf_op jit(solution)/shard_map/ppermute | solution.py:19
  34.8 1.3 fusion.18
  36.1 1.6 slice_subtract_fusion.3
  37.7 1.6 slice_subtract_fusion.2
  39.3 0.7 fusion.34
  40.2 3.5 %collective-permute-start.9 = (f32[32,4,256]{2,1,0:T(4,128)S(1)}, f32[32,4,256]{2,1,0:T(4,128)S(1)}, u32[]{:S(2)}, u32[]{:S(2)}) collective-permute-start(f32[32,4,256]{2,1,0:T(4,128)S(1)} %get-tuple-element.58), channel_id=1, source_target_pairs={{2,0},{4,2},{6,4},{8,6},{10,8},{12,10},{14,12},{0,14},{3,1},{5,3},... | collective-permute-start | bytes 393224 | tf_op jit(solution)/shard_map/ppermute | solution.py:19
  44.0 3.5 %collective-permute-start.13 = (f32[32,4,256]{2,1,0:T(4,128)S(1)}, f32[32,4,256]{2,1,0:T(4,128)S(1)}, u32[]{:S(2)}, u32[]{:S(2)}) collective-permute-start(f32[32,4,256]{2,1,0:T(4,128)S(1)} %get-tuple-element.48), channel_id=1, source_target_pairs={{2,0},{4,2},{6,4},{8,6},{10,8},{12,10},{14,12},{0,14},{3,1},{5,3},... | collective-permute-start | bytes 393224 | tf_op jit(solution)/shard_map/ppermute | solution.py:19
  48.4 1.8 %collective-permute-start.11 = (f32[32,24,4]{2,1,0:T(8,128)S(1)}, f32[32,24,4]{2,1,0:T(8,128)S(1)}, u32[]{:S(2)}, u32[]{:S(2)}) collective-permute-start(f32[32,24,4]{2,1,0:T(8,128)S(1)} %get-tuple-element.54), channel_id=1, source_target_pairs={{1,0},{0,1},{3,2},{2,3},{5,4},{4,5},{7,6},{6,7},{9,8},{8,9},{11,10... | collective-permute-start | bytes 36872 | tf_op jit(solution)/shard_map/ppermute | solution.py:19
  50.6 0.8 collective-permute-start.14
  51.3 1.3 collective-permute-start.15
  52.7 7.5 %collective-permute-done.10 = f32[32,24,4]{2,1,0:T(8,128)S(1)} collective-permute-done((f32[32,24,4]{2,1,0:T(8,128)S(1)}, f32[32,24,4]{2,1,0:T(8,128)S(1)}, u32[]{:S(2)}, u32[]{:S(2)}) %collective-permute-start.10) | collective-permute-done | bytes 12320 | tf_op jit(solution)/shard_map/ppermute | solution.py:16
  60.1 8.4 %collective-permute-done.11 = f32[32,24,4]{2,1,0:T(8,128)S(1)} collective-permute-done((f32[32,24,4]{2,1,0:T(8,128)S(1)}, f32[32,24,4]{2,1,0:T(8,128)S(1)}, u32[]{:S(2)}, u32[]{:S(2)}) %collective-permute-start.11) | collective-permute-done | bytes 12320 | tf_op jit(solution)/shard_map/ppermute | solution.py:19
  68.6 0.7 pad_maximum_fusion.5
  69.3 7.7 %collective-permute-done.14 = f32[32,24,4]{2,1,0:T(8,128)S(1)} collective-permute-done((f32[32,24,4]{2,1,0:T(8,128)S(1)}, f32[32,24,4]{2,1,0:T(8,128)S(1)}, u32[]{:S(2)}, u32[]{:S(2)}) %collective-permute-start.14) | collective-permute-done | bytes 12320 | tf_op jit(solution)/shard_map/ppermute | solution.py:16
  77.0 4.4 %collective-permute-done.15 = f32[32,24,4]{2,1,0:T(8,128)S(1)} collective-permute-done((f32[32,24,4]{2,1,0:T(8,128)S(1)}, f32[32,24,4]{2,1,0:T(8,128)S(1)}, u32[]{:S(2)}, u32[]{:S(2)}) %collective-permute-start.15) | collective-permute-done | bytes 12320 | tf_op jit(solution)/shard_map/ppermute | solution.py:19
  81.4 2.1 %fusion.6 = f32[32,22,262]{2,1,0:T(8,128)S(1)} fusion(f32[32,24,4]{2,1,0:T(8,128)S(1)} %collective-permute-done.15, f32[32,24,4]{2,1,0:T(8,128)S(1)} %collective-permute-done.14, f32[32,4,256]{2,1,0:T(4,128)S(1)} %collective-permute-done.13, f32[32,16,256]{2,1,0:T(8,128)S(1)} %get-tuple-element.49, f32[32,4,256]{2,1,0:T(4,128)S(1)} %collective-permute-done.12, ...), kind=kLoop, calls=%fused_computation.15 | loop fusion | flops 2028928 | bytes 5266580 | tf_op jit(solution)/shard_map/sub | solution.py:76
  83.5 1.6 slice_subtract_fusion.1
  85.1 1.6 slice_subtract_fusion
  86.7 1.3 multiply_reduce_fusion.8
  88.1 1.6 %multiply_reduce_fusion.1 = (f32[]{:T(128)}, f32[]{:T(128)}, f32[]{:T(128)}, f32[]{:T(128)}, f32[]{:T(128)}, /*index=5*/f32[]{:T(128)}, f32[]{:T(128)}, f32[]{:T...) fusion(f32[32,16,256]{2,1,0:T(8,128)S(1)} %get-tuple-element.46, ...), kind=kLoop, calls=%fused_computation.63 | loop fusion | flops 4194288 | bytes 4718656 | tf_op jit(solution)/shard_map/reduce_sum | solution.py:82
  89.7 40.1 %all-reduce = (f32[1]{0:T(128)}, f32[1]{0:T(128)}, f32[1]{0:T(128)}, f32[1]{0:T(128)}, f32[1]{0:T(128)}, /*index=5*/f32[1]{0:T(128)}, f32[1]{0:T(128)}, f32[1]{0...) all-reduce(f32[1]{0:T(128)} %bitcast, f32[1]{0:T(128)} %bitcast.1, ...), channel_id=1, replica_groups=mesh['grp'=2,'row'=8,'col'=2] {'grp','row','col'}, use_global_device_ids=true, to_apply=%region_1.2 | all-reduce | flops 17 | bytes 136 | tf_op jit(solution)/shard_map/psum | solution.py:84
  129.8 5.7 %stack.84 = f32[9]{0:T(128)S(1)} concatenate(f32[1]{0:T(128)} %get-tuple-element.27, f32[1]{0:T(128)} %get-tuple-element.28, f32[1]{0:T(128)} %get-tuple-element.29, f32[1]{0:T(128)} %get-tuple-element.30, f32[1]{0:T(128)} %get-tuple-element.31, f32[1]{0:T(128)} %get-tuple-element.32, f32[1]{0:T(128)} %get-tuple-element.33, f32[1]{0:T(128)} %get-tuple-element.34, f32[1]{0:T(128)} %get-tuple-element.35), dimensions={0} | concatenate | bytes 72 | tf_op jit(solution)/shard_map/stack | solution.py:90
  135.5 5.2 %stack.93 = f32[8]{0:T(128)S(1)} concatenate(f32[1]{0:T(128)} %get-tuple-element.36, f32[1]{0:T(128)} %get-tuple-element.37, f32[1]{0:T(128)} %get-tuple-element.38, f32[1]{0:T(128)} %get-tuple-element.39, f32[1]{0:T(128)} %get-tuple-element.40, f32[1]{0:T(128)} %get-tuple-element.41, f32[1]{0:T(128)} %get-tuple-element.42, f32[1]{0:T(128)} %get-tuple-element.43), dimensions={0} | concatenate | bytes 64 | tf_op jit(solution)/shard_map/stack | solution.py:91
  160.2 1.9 %stack.94 = f32[17]{0:T(128)} concatenate(f32[1]{0:T(128)} %get-tuple-element.73, f32[1]{0:T(128)} %get-tuple-element.82, f32[1]{0:T(128)S(6)} %sub.120, f32[1]{0:T(128)S(6)} %sub.121, f32[1]{0:T(128)S(6)} %sub.122, f32[1]{0:T(128)S(6)} %sub.123, f32[1]{0:T(128)S(6)} %sub.124, f32[1]{0:T(128)S(6)} %sub.125, f32[1]{0:T(128)S(6)} %sub.126, f32[1]{0:T(128)S(6)} %sub.127, ...), dimensions={0} | concatenate | bytes 136 | tf_op jit(solution)/shard_map/stack | solution.py:101
  (47 shorter events, 5.4 us)
Async XLA Ops:
  1.4 9.6 %collective-permute-start = (f32[4,256]{1,0:T(4,128)S(1)}, f32[4,256]{1,0:T(4,128)S(1)}, u32[]{:S(2)}, u32[]{:S(2)}) collective-permute-start(f32[4,256]{1,0:T(4,128)S(1)} %get-tuple-element.63), channel_id=1, source_target_pairs={{0,2},{2,4},{4,6},{6,8},{8,10},{10,12},{12,14},{14,0},{1,3},{3,5},... | collective-permute-start | bytes 12296 | tf_op jit(solution)/shard_map/ppermute | solution.py:16
  1.8 9.1 %collective-permute-start.1 = (f32[4,256]{1,0:T(4,128)S(1)}, f32[4,256]{1,0:T(4,128)S(1)}, u32[]{:S(2)}, u32[]{:S(2)}) collective-permute-start(f32[4,256]{1,0:T(4,128)S(1)} %get-tuple-element.64), channel_id=1, source_target_pairs={{2,0},{4,2},{6,4},{8,6},{10,8},{12,10},{14,12},{0,14},{3,1},{5,3},... | collective-permute-start | bytes 12296 | tf_op jit(solution)/shard_map/ppermute | solution.py:19
  7.0 6.9 %collective-permute-start.4 = (f32[32,4,256]{2,1,0:T(4,128)S(1)}, f32[32,4,256]{2,1,0:T(4,128)S(1)}, u32[]{:S(2)}, u32[]{:S(2)}) collective-permute-start(f32[32,4,256]{2,1,0:T(4,128)S(1)} %get-tuple-element.59), channel_id=1, source_target_pairs={{0,2},{2,4},{4,6},{6,8},{8,10},{10,12},{12,14},{14,0},{1,3},{3,5},... | collective-permute-start | bytes 393224 | tf_op jit(solution)/shard_map/ppermute | solution.py:16
  7.0 6.8 %collective-permute-start.5 = (f32[32,4,256]{2,1,0:T(4,128)S(1)}, f32[32,4,256]{2,1,0:T(4,128)S(1)}, u32[]{:S(2)}, u32[]{:S(2)}) collective-permute-start(f32[32,4,256]{2,1,0:T(4,128)S(1)} %get-tuple-element.60), channel_id=1, source_target_pairs={{2,0},{4,2},{6,4},{8,6},{10,8},{12,10},{14,12},{0,14},{3,1},{5,3},... | collective-permute-start | bytes 393224 | tf_op jit(solution)/shard_map/ppermute | solution.py:19
  11.7 6.1 %collective-permute-start.2 = (f32[24,4]{1,0:T(8,128)S(1)}, f32[24,4]{1,0:T(8,128)S(1)}, u32[]{:S(2)}, u32[]{:S(2)}) collective-permute-start(f32[24,4]{1,0:T(8,128)S(1)} %get-tuple-element.61), channel_id=1, source_target_pairs={{0,1},{1,0},{2,3},{3,2},{4,5},{5,4},{6,7},{7,6},{8,9},{9,8},{10,11... | collective-permute-start | bytes 1160 | tf_op jit(solution)/shard_map/ppermute | solution.py:16
  13.7 4.1 %collective-permute-start.3 = (f32[24,4]{1,0:T(8,128)S(1)}, f32[24,4]{1,0:T(8,128)S(1)}, u32[]{:S(2)}, u32[]{:S(2)}) collective-permute-start(f32[24,4]{1,0:T(8,128)S(1)} %get-tuple-element.62), channel_id=1, source_target_pairs={{1,0},{0,1},{3,2},{2,3},{5,4},{4,5},{7,6},{6,7},{9,8},{8,9},{11,10... | collective-permute-start | bytes 1160 | tf_op jit(solution)/shard_map/ppermute | solution.py:19
  15.0 2.8 %copy-start.3 = (f32[16,256]{1,0:T(8,128)S(1)}, f32[16,256]{1,0:T(8,128)}, u32[]{:S(2)}) copy-start(f32[16,256]{1,0:T(8,128)} %param.3) | copy-start | bytes 49156
  15.0 19.1 %copy-start = (f32[32,16,256]{2,1,0:T(8,128)S(1)}, f32[32,16,256]{2,1,0:T(8,128)}, u32[]{:S(2)}) copy-start(f32[32,16,256]{2,1,0:T(8,128)} %param.2) | copy-start | bytes 1572868
  15.2 12.5 %collective-permute-start.6 = (f32[32,24,4]{2,1,0:T(8,128)S(1)}, f32[32,24,4]{2,1,0:T(8,128)S(1)}, u32[]{:S(2)}, u32[]{:S(2)}) collective-permute-start(f32[32,24,4]{2,1,0:T(8,128)S(1)} %get-tuple-element.55), channel_id=1, source_target_pairs={{0,1},{1,0},{2,3},{3,2},{4,5},{5,4},{6,7},{7,6},{8,9},{9,8},{10,11... | collective-permute-start | bytes 36872 | tf_op jit(solution)/shard_map/ppermute | solution.py:16
  17.7 16.3 %collective-permute-start.7 = (f32[32,24,4]{2,1,0:T(8,128)S(1)}, f32[32,24,4]{2,1,0:T(8,128)S(1)}, u32[]{:S(2)}, u32[]{:S(2)}) collective-permute-start(f32[32,24,4]{2,1,0:T(8,128)S(1)} %get-tuple-element.56), channel_id=1, source_target_pairs={{1,0},{0,1},{3,2},{2,3},{5,4},{4,5},{7,6},{6,7},{9,8},{8,9},{11,10... | collective-permute-start | bytes 36872 | tf_op jit(solution)/shard_map/ppermute | solution.py:19
  40.1 7.6 %collective-permute-start.8 = (f32[32,4,256]{2,1,0:T(4,128)S(1)}, f32[32,4,256]{2,1,0:T(4,128)S(1)}, u32[]{:S(2)}, u32[]{:S(2)}) collective-permute-start(f32[32,4,256]{2,1,0:T(4,128)S(1)} %get-tuple-element.57), channel_id=1, source_target_pairs={{0,2},{2,4},{4,6},{6,8},{8,10},{10,12},{12,14},{14,0},{1,3},{3,5},... | collective-permute-start | bytes 393224 | tf_op jit(solution)/shard_map/ppermute | solution.py:16
  40.2 7.6 %collective-permute-start.9 = (f32[32,4,256]{2,1,0:T(4,128)S(1)}, f32[32,4,256]{2,1,0:T(4,128)S(1)}, u32[]{:S(2)}, u32[]{:S(2)}) collective-permute-start(f32[32,4,256]{2,1,0:T(4,128)S(1)} %get-tuple-element.58), channel_id=1, source_target_pairs={{2,0},{4,2},{6,4},{8,6},{10,8},{12,10},{14,12},{0,14},{3,1},{5,3},... | collective-permute-start | bytes 393224 | tf_op jit(solution)/shard_map/ppermute | solution.py:19
  43.9 6.3 %collective-permute-start.12 = (f32[32,4,256]{2,1,0:T(4,128)S(1)}, f32[32,4,256]{2,1,0:T(4,128)S(1)}, u32[]{:S(2)}, u32[]{:S(2)}) collective-permute-start(f32[32,4,256]{2,1,0:T(4,128)S(1)} %get-tuple-element.47), channel_id=1, source_target_pairs={{0,2},{2,4},{4,6},{6,8},{8,10},{10,12},{12,14},{14,0},{1,3},{3,5},... | collective-permute-start | bytes 393224 | tf_op jit(solution)/shard_map/ppermute | solution.py:16
  44.0 6.3 %collective-permute-start.13 = (f32[32,4,256]{2,1,0:T(4,128)S(1)}, f32[32,4,256]{2,1,0:T(4,128)S(1)}, u32[]{:S(2)}, u32[]{:S(2)}) collective-permute-start(f32[32,4,256]{2,1,0:T(4,128)S(1)} %get-tuple-element.48), channel_id=1, source_target_pairs={{2,0},{4,2},{6,4},{8,6},{10,8},{12,10},{14,12},{0,14},{3,1},{5,3},... | collective-permute-start | bytes 393224 | tf_op jit(solution)/shard_map/ppermute | solution.py:19
  48.1 12.1 %collective-permute-start.10 = (f32[32,24,4]{2,1,0:T(8,128)S(1)}, f32[32,24,4]{2,1,0:T(8,128)S(1)}, u32[]{:S(2)}, u32[]{:S(2)}) collective-permute-start(f32[32,24,4]{2,1,0:T(8,128)S(1)} %get-tuple-element.53), channel_id=1, source_target_pairs={{0,1},{1,0},{2,3},{3,2},{4,5},{5,4},{6,7},{7,6},{8,9},{9,8},{10,11... | collective-permute-start | bytes 36872 | tf_op jit(solution)/shard_map/ppermute | solution.py:16
  48.4 20.2 %collective-permute-start.11 = (f32[32,24,4]{2,1,0:T(8,128)S(1)}, f32[32,24,4]{2,1,0:T(8,128)S(1)}, u32[]{:S(2)}, u32[]{:S(2)}) collective-permute-start(f32[32,24,4]{2,1,0:T(8,128)S(1)} %get-tuple-element.54), channel_id=1, source_target_pairs={{1,0},{0,1},{3,2},{2,3},{5,4},{4,5},{7,6},{6,7},{9,8},{8,9},{11,10... | collective-permute-start | bytes 36872 | tf_op jit(solution)/shard_map/ppermute | solution.py:19
  50.6 26.4 %collective-permute-start.14 = (f32[32,24,4]{2,1,0:T(8,128)S(1)}, f32[32,24,4]{2,1,0:T(8,128)S(1)}, u32[]{:S(2)}, u32[]{:S(2)}) collective-permute-start(f32[32,24,4]{2,1,0:T(8,128)S(1)} %get-tuple-element.51), channel_id=1, source_target_pairs={{0,1},{1,0},{2,3},{3,2},{4,5},{5,4},{6,7},{7,6},{8,9},{9,8},{10,11... | collective-permute-start | bytes 36872 | tf_op jit(solution)/shard_map/ppermute | solution.py:16
  51.3 30.1 %collective-permute-start.15 = (f32[32,24,4]{2,1,0:T(8,128)S(1)}, f32[32,24,4]{2,1,0:T(8,128)S(1)}, u32[]{:S(2)}, u32[]{:S(2)}) collective-permute-start(f32[32,24,4]{2,1,0:T(8,128)S(1)} %get-tuple-element.52), channel_id=1, source_target_pairs={{1,0},{0,1},{3,2},{2,3},{5,4},{4,5},{7,6},{6,7},{9,8},{8,9},{11,10... | collective-permute-start | bytes 36872 | tf_op jit(solution)/shard_map/ppermute | solution.py:19
  88.1 1.7 %copy-start.1 = (f32[32,16,256]{2,1,0:T(8,128)}, f32[32,16,256]{2,1,0:T(8,128)S(1)}, u32[]{:S(2)}) copy-start(f32[32,16,256]{2,1,0:T(8,128)S(1)} %get-tuple-element.45) | copy-start | bytes 1572868
  88.1 1.7 %copy-start.2 = (f32[32,16,256]{2,1,0:T(8,128)}, f32[32,16,256]{2,1,0:T(8,128)S(1)}, u32[]{:S(2)}) copy-start(f32[32,16,256]{2,1,0:T(8,128)S(1)} %get-tuple-element.46) | copy-start | bytes 1572868
where the time goes:
time: 163 us; the launch traced here: 162 us
  waiting for transfers between devices  44.3 us (27%)
  blocking collectives  40.1 us (25%)
  starting transfers between devices  24.2 us (15%)
  between operations  19.6 us (12%)
  other arithmetic  17.3 us (11%)
  local copies, waits for them, and re-layouts  16.7 us (10%)
    psum x1, blocking collectives, body(): total_squares = [lax.psum(squares[0], ('grp', 'row', 'col'))]  40.1 us
    ppermute x8, waiting for transfers between devices, extended(): lax.ppermute(lax.slice_in_dim(block, block.shape[dim] - width, None, axis...  25.1 us
    ppermute x8, waiting for transfers between devices, extended(): lax.ppermute(lax.slice_in_dim(block, 0, width, axis=dim), axis, backward)  19.2 us
    ppermute x8, starting transfers between devices, extended(): lax.ppermute(lax.slice_in_dim(block, 0, width, axis=dim), axis, backward)  17.9 us
    sub x5, other arithmetic, body(): latest = 2.0 * advance(padded_new) - padded_old[:, 1:-1, 1:-1]  8.54 us
    ppermute x8, starting transfers between devices, extended(): lax.ppermute(lax.slice_in_dim(block, block.shape[dim] - width, None, axis...  6.28 us
    another operation x1, local copies, waits for them, and re-layouts, body(): total_squares = jnp.stack(total_squares)  5.71 us
    another operation x1, local copies, waits for them, and re-layouts, body(): total_crosses = jnp.stack(total_crosses)  5.19 us
  transfers between devices with their start and end apart: 16, of which 8 were waited for; matrix products, arithmetic and copies ran while one was open for 3% of the time, Pallas kernels for 0%

commit v1 on v0

--- a/solution.py
+++ b/solution.py
@@ -81,7 +81,13 @@
             squares.append(jnp.sum(kept_new * kept_new))
             crosses.append(jnp.sum(kept_new * kept_old))
         older, newer = (padded_old, padded_new)
-    total_squares = [lax.psum(squares[0], ("grp", "row", "col"))]
+
+    def turns_drive(unit, axis_id, bus_axis):
+        for j in (axis_id, bus_axis):
+            unit = jax.lax.psum(unit, axis_name=j)
+        return unit
+
+    total_squares = [turns_drive(squares[0], ("row", "col"), "grp")]
     total_crosses = []
     for index in range(STEPS):
         pair = lax.psum((squares[index + 1], crosses[index]), ("grp", "row", "col"))

time: 163 us -> 200 us (1.23)
  blocking collectives: 40.1 us -> 75.8 us
    psum x1 -> x3, blocking collectives: 40.1 us -> 75.8 us  [the longest x2 38.4 us: turns_drive(): unit = jax.lax.psum(unit, axis_name=j)]
where the time goes in v1:
time: 200 us; the launch traced here: 198 us
  blocking collectives  75.8 us (38%)
  waiting for transfers between devices  44.3 us (22%)
  starting transfers between devices  24.2 us (12%)
  between operations  19.6 us (10%)
  other arithmetic  17.3 us (9%)
  local copies, waits for them, and re-layouts  16.7 us (8%)
    psum x2, blocking collectives, turns_drive(): unit = jax.lax.psum(unit, axis_name=j)  38.4 us
    psum x1, blocking collectives, body(): pair = lax.psum((squares[index + 1], crosses[index]), ('grp', 'row', 'col'))  37.4 us
    ppermute x8, waiting for transfers between devices, extended(): lax.ppermute(lax.slice_in_dim(block, block.shape[dim] - width, None, axis...  25.1 us
    ppermute x8, waiting for transfers between devices, extended(): lax.ppermute(lax.slice_in_dim(block, 0, width, axis=dim), axis, backward)  19.2 us
    ppermute x8, starting transfers between devices, extended(): lax.ppermute(lax.slice_in_dim(block, 0, width, axis=dim), axis, backward)  17.9 us
    sub x5, other arithmetic, body(): latest = 2.0 * advance(padded_new) - padded_old[:, 1:-1, 1:-1]  8.54 us
    ppermute x8, starting transfers between devices, extended(): lax.ppermute(lax.slice_in_dim(block, block.shape[dim] - width, None, axis...  6.28 us
    another operation x1, local copies, waits for them, and re-layouts, body(): total_squares = jnp.stack(total_squares)  5.71 us
  transfers between devices with their start and end apart: 16, of which 8 were waited for; matrix products, arithmetic and copies ran while one was open for 3% of the time, Pallas kernels for 0%

profile of v1, /device:TPU:0, one launch (start us, length us, event | category | flops | bytes accessed | tf_op | source)
XLA Modules:
  0.0 197.8 jit_solution(1050548068692872570)
XLA Ops:
  1.8 4.0 %collective-permute-start.1 = (f32[4,256]{1,0:T(4,128)S(1)}, f32[4,256]{1,0:T(4,128)S(1)}, u32[]{:S(2)}, u32[]{:S(2)}) collective-permute-start(f32[4,256]{1,0:T(4,128)S(1)} %get-tuple-element.63), channel_id=1, source_target_pairs={{2,0},{4,2},{6,4},{8,6},{10,8},{12,10},{14,12},{0,14},{3,1},{5,3},... | collective-permute-start | bytes 12296 | tf_op jit(solution)/shard_map/ppermute | solution.py:19
  5.9 1.1 fusion.39
  7.0 3.5 %collective-permute-start.5 = (f32[32,4,256]{2,1,0:T(4,128)S(1)}, f32[32,4,256]{2,1,0:T(4,128)S(1)}, u32[]{:S(2)}, u32[]{:S(2)}) collective-permute-start(f32[32,4,256]{2,1,0:T(4,128)S(1)} %get-tuple-element.59), channel_id=1, source_target_pairs={{2,0},{4,2},{6,4},{8,6},{10,8},{12,10},{14,12},{0,14},{3,1},{5,3},... | collective-permute-start | bytes 393224 | tf_op jit(solution)/shard_map/ppermute | solution.py:19
  11.7 2.0 %collective-permute-start.2 = (f32[24,4]{1,0:T(8,128)S(1)}, f32[24,4]{1,0:T(8,128)S(1)}, u32[]{:S(2)}, u32[]{:S(2)}) collective-permute-start(f32[24,4]{1,0:T(8,128)S(1)} %get-tuple-element.60), channel_id=1, source_target_pairs={{0,1},{1,0},{2,3},{3,2},{4,5},{5,4},{6,7},{7,6},{8,9},{9,8},{10,11... | collective-permute-start | bytes 1160 | tf_op jit(solution)/shard_map/ppermute | solution.py:16
  13.8 1.2 pad_maximum_fusion.6
  15.2 2.6 %collective-permute-start.6 = (f32[32,24,4]{2,1,0:T(8,128)S(1)}, f32[32,24,4]{2,1,0:T(8,128)S(1)}, u32[]{:S(2)}, u32[]{:S(2)}) collective-permute-start(f32[32,24,4]{2,1,0:T(8,128)S(1)} %get-tuple-element.54), channel_id=1, source_target_pairs={{0,1},{1,0},{2,3},{3,2},{4,5},{5,4},{6,7},{7,6},{8,9},{9,8},{10,11... | collective-permute-start | bytes 36872 | tf_op jit(solution)/shard_map/ppermute | solution.py:16
  18.2 9.5 %collective-permute-done.6 = f32[32,24,4]{2,1,0:T(8,128)S(1)} collective-permute-done((f32[32,24,4]{2,1,0:T(8,128)S(1)}, f32[32,24,4]{2,1,0:T(8,128)S(1)}, u32[]{:S(2)}, u32[]{:S(2)}) %collective-permute-start.6) | collective-permute-done | bytes 12320 | tf_op jit(solution)/shard_map/ppermute | solution.py:16
  27.7 6.4 %collective-permute-done.7 = f32[32,24,4]{2,1,0:T(8,128)S(1)} collective-permute-done((f32[32,24,4]{2,1,0:T(8,128)S(1)}, f32[32,24,4]{2,1,0:T(8,128)S(1)}, u32[]{:S(2)}, u32[]{:S(2)}) %collective-permute-start.7) | collective-permute-done | bytes 12320 | tf_op jit(solution)/shard_map/ppermute | solution.py:19
  34.8 1.3 fusion.18
  36.1 1.6 slice_subtract_fusion.3
  37.7 1.6 slice_subtract_fusion.2
  39.3 0.7 fusion.34
  40.2 3.5 %collective-permute-start.9 = (f32[32,4,256]{2,1,0:T(4,128)S(1)}, f32[32,4,256]{2,1,0:T(4,128)S(1)}, u32[]{:S(2)}, u32[]{:S(2)}) collective-permute-start(f32[32,4,256]{2,1,0:T(4,128)S(1)} %get-tuple-element.57), channel_id=1, source_target_pairs={{2,0},{4,2},{6,4},{8,6},{10,8},{12,10},{14,12},{0,14},{3,1},{5,3},... | collective-permute-start | bytes 393224 | tf_op jit(solution)/shard_map/ppermute | solution.py:19
  44.0 3.5 %collective-permute-start.13 = (f32[32,4,256]{2,1,0:T(4,128)S(1)}, f32[32,4,256]{2,1,0:T(4,128)S(1)}, u32[]{:S(2)}, u32[]{:S(2)}) collective-permute-start(f32[32,4,256]{2,1,0:T(4,128)S(1)} %get-tuple-element.47), channel_id=1, source_target_pairs={{2,0},{4,2},{6,4},{8,6},{10,8},{12,10},{14,12},{0,14},{3,1},{5,3},... | collective-permute-start | bytes 393224 | tf_op jit(solution)/shard_map/ppermute | solution.py:19
  48.4 1.8 collective-permute-start.11
  50.6 0.8 collective-permute-start.14
  51.3 1.3 collective-permute-start.15
  52.7 7.5 %collective-permute-done.10 = f32[32,24,4]{2,1,0:T(8,128)S(1)} collective-permute-done((f32[32,24,4]{2,1,0:T(8,128)S(1)}, f32[32,24,4]{2,1,0:T(8,128)S(1)}, u32[]{:S(2)}, u32[]{:S(2)}) %collective-permute-start.10) | collective-permute-done | bytes 12320 | tf_op jit(solution)/shard_map/ppermute | solution.py:16
  60.1 8.4 %collective-permute-done.11 = f32[32,24,4]{2,1,0:T(8,128)S(1)} collective-permute-done((f32[32,24,4]{2,1,0:T(8,128)S(1)}, f32[32,24,4]{2,1,0:T(8,128)S(1)}, u32[]{:S(2)}, u32[]{:S(2)}) %collective-permute-start.11) | collective-permute-done | bytes 12320 | tf_op jit(solution)/shard_map/ppermute | solution.py:19
  69.3 7.7 %collective-permute-done.14 = f32[32,24,4]{2,1,0:T(8,128)S(1)} collective-permute-done((f32[32,24,4]{2,1,0:T(8,128)S(1)}, f32[32,24,4]{2,1,0:T(8,128)S(1)}, u32[]{:S(2)}, u32[]{:S(2)}) %collective-permute-start.14) | collective-permute-done | bytes 12320 | tf_op jit(solution)/shard_map/ppermute | solution.py:16
  77.0 4.4 %collective-permute-done.15 = f32[32,24,4]{2,1,0:T(8,128)S(1)} collective-permute-done((f32[32,24,4]{2,1,0:T(8,128)S(1)}, f32[32,24,4]{2,1,0:T(8,128)S(1)}, u32[]{:S(2)}, u32[]{:S(2)}) %collective-permute-start.15) | collective-permute-done | bytes 12320 | tf_op jit(solution)/shard_map/ppermute | solution.py:19
  81.4 2.1 %fusion.6 = f32[32,22,262]{2,1,0:T(8,128)S(1)} fusion(f32[32,24,4]{2,1,0:T(8,128)S(1)} %collective-permute-done.15, f32[32,24,4]{2,1,0:T(8,128)S(1)} %collective-permute-done.14, f32[32,4,256]{2,1,0:T(4,128)S(1)} %collective-permute-done.13, f32[32,16,256]{2,1,0:T(8,128)S(1)} %get-tuple-element.48, f32[32,4,256]{2,1,0:T(4,128)S(1)} %collective-permute-done.12, ...), kind=kLoop, calls=%fused_computation.15 | loop fusion | flops 2028928 | bytes 5266580 | tf_op jit(solution)/shard_map/sub | solution.py:76
  83.5 1.6 slice_subtract_fusion.1
  85.1 1.6 slice_subtract_fusion
  86.7 1.3 multiply_reduce_fusion.8
  88.1 1.7 multiply_reduce_fusion.1
  89.7 32.8 %psum.126 = f32[]{:T(128)} all-reduce(f32[]{:T(128)} %get-tuple-element.16), channel_id=1, replica_groups=mesh['grp'=2,'row'=8,'col'=2] {'row','col'}, use_global_device_ids=true, to_apply=%region_1.2 | all-reduce | flops 1 | bytes 8 | tf_op jit(solution)/shard_map/psum | solution.py:87
  122.6 5.6 %psum.127 = f32[1]{0:T(128)} all-reduce(f32[1]{0:T(128)} %bitcast), channel_id=1, replica_groups=mesh['grp'=2,'row'=8,'col'=2] {'grp'}, use_global_device_ids=true, to_apply=%region_2.3 | all-reduce | flops 1 | bytes 8 | tf_op jit(solution)/shard_map/psum | solution.py:87
  128.1 37.4 %all-reduce = (f32[1]{0:T(128)}, f32[1]{0:T(128)}, f32[1]{0:T(128)}, f32[1]{0:T(128)}, f32[1]{0:T(128)}, /*index=5*/f32[1]{0:T(128)}, f32[1]{0:T(128)}, f32[1]{0...) all-reduce(f32[1]{0:T(128)} %bitcast.1, ...), channel_id=1, replica_groups=mesh['grp'=2,'row'=8,'col'=2] {'grp','row','col'}, use_global_device_ids=true, to_apply=%region_4.5 | all-reduce | flops 16 | bytes 128 | tf_op jit(solution)/shard_map/psum | solution.py:93
  165.6 5.7 %stack.84 = f32[9]{0:T(128)S(1)} concatenate(f32[1]{0:T(128)} %psum.127, f32[1]{0:T(128)} %get-tuple-element.27, f32[1]{0:T(128)} %get-tuple-element.28, f32[1]{0:T(128)} %get-tuple-element.29, f32[1]{0:T(128)} %get-tuple-element.30, f32[1]{0:T(128)} %get-tuple-element.31, f32[1]{0:T(128)} %get-tuple-element.32, f32[1]{0:T(128)} %get-tuple-element.33, f32[1]{0:T(128)} %get-tuple-element.34), dimensions={0} | concatenate | bytes 72 | tf_op jit(solution)/shard_map/stack | solution.py:96
  171.3 5.2 %stack.93 = f32[8]{0:T(128)S(1)} concatenate(f32[1]{0:T(128)} %get-tuple-element.35, f32[1]{0:T(128)} %get-tuple-element.36, f32[1]{0:T(128)} %get-tuple-element.37, f32[1]{0:T(128)} %get-tuple-element.38, f32[1]{0:T(128)} %get-tuple-element.39, f32[1]{0:T(128)} %get-tuple-element.40, f32[1]{0:T(128)} %get-tuple-element.41, f32[1]{0:T(128)} %get-tuple-element.42), dimensions={0} | concatenate | bytes 64 | tf_op jit(solution)/shard_map/stack | solution.py:97
  196.0 1.9 stack.94
  (49 shorter events, 6.9 us)
Async XLA Ops:
  1.4 9.6 %collective-permute-start = (f32[4,256]{1,0:T(4,128)S(1)}, f32[4,256]{1,0:T(4,128)S(1)}, u32[]{:S(2)}, u32[]{:S(2)}) collective-permute-start(f32[4,256]{1,0:T(4,128)S(1)} %get-tuple-element.62), channel_id=1, source_target_pairs={{0,2},{2,4},{4,6},{6,8},{8,10},{10,12},{12,14},{14,0},{1,3},{3,5},... | collective-permute-start | bytes 12296 | tf_op jit(solution)/shard_map/ppermute | solution.py:16
  1.8 9.1 %collective-permute-start.1 = (f32[4,256]{1,0:T(4,128)S(1)}, f32[4,256]{1,0:T(4,128)S(1)}, u32[]{:S(2)}, u32[]{:S(2)}) collective-permute-start(f32[4,256]{1,0:T(4,128)S(1)} %get-tuple-element.63), channel_id=1, source_target_pairs={{2,0},{4,2},{6,4},{8,6},{10,8},{12,10},{14,12},{0,14},{3,1},{5,3},... | collective-permute-start | bytes 12296 | tf_op jit(solution)/shard_map/ppermute | solution.py:19
  7.0 6.9 %collective-permute-start.4 = (f32[32,4,256]{2,1,0:T(4,128)S(1)}, f32[32,4,256]{2,1,0:T(4,128)S(1)}, u32[]{:S(2)}, u32[]{:S(2)}) collective-permute-start(f32[32,4,256]{2,1,0:T(4,128)S(1)} %get-tuple-element.58), channel_id=1, source_target_pairs={{0,2},{2,4},{4,6},{6,8},{8,10},{10,12},{12,14},{14,0},{1,3},{3,5},... | collective-permute-start | bytes 393224 | tf_op jit(solution)/shard_map/ppermute | solution.py:16
  7.0 6.8 %collective-permute-start.5 = (f32[32,4,256]{2,1,0:T(4,128)S(1)}, f32[32,4,256]{2,1,0:T(4,128)S(1)}, u32[]{:S(2)}, u32[]{:S(2)}) collective-permute-start(f32[32,4,256]{2,1,0:T(4,128)S(1)} %get-tuple-element.59), channel_id=1, source_target_pairs={{2,0},{4,2},{6,4},{8,6},{10,8},{12,10},{14,12},{0,14},{3,1},{5,3},... | collective-permute-start | bytes 393224 | tf_op jit(solution)/shard_map/ppermute | solution.py:19
  11.7 6.1 %collective-permute-start.2 = (f32[24,4]{1,0:T(8,128)S(1)}, f32[24,4]{1,0:T(8,128)S(1)}, u32[]{:S(2)}, u32[]{:S(2)}) collective-permute-start(f32[24,4]{1,0:T(8,128)S(1)} %get-tuple-element.60), channel_id=1, source_target_pairs={{0,1},{1,0},{2,3},{3,2},{4,5},{5,4},{6,7},{7,6},{8,9},{9,8},{10,11... | collective-permute-start | bytes 1160 | tf_op jit(solution)/shard_map/ppermute | solution.py:16
  13.7 4.1 %collective-permute-start.3 = (f32[24,4]{1,0:T(8,128)S(1)}, f32[24,4]{1,0:T(8,128)S(1)}, u32[]{:S(2)}, u32[]{:S(2)}) collective-permute-start(f32[24,4]{1,0:T(8,128)S(1)} %get-tuple-element.61), channel_id=1, source_target_pairs={{1,0},{0,1},{3,2},{2,3},{5,4},{4,5},{7,6},{6,7},{9,8},{8,9},{11,10... | collective-permute-start | bytes 1160 | tf_op jit(solution)/shard_map/ppermute | solution.py:19
  15.0 2.8 %copy-start.3 = (f32[16,256]{1,0:T(8,128)S(1)}, f32[16,256]{1,0:T(8,128)}, u32[]{:S(2)}) copy-start(f32[16,256]{1,0:T(8,128)} %param.3) | copy-start | bytes 49156
  15.0 19.1 %copy-start = (f32[32,16,256]{2,1,0:T(8,128)S(1)}, f32[32,16,256]{2,1,0:T(8,128)}, u32[]{:S(2)}) copy-start(f32[32,16,256]{2,1,0:T(8,128)} %param.2) | copy-start | bytes 1572868
  15.2 12.5 %collective-permute-start.6 = (f32[32,24,4]{2,1,0:T(8,128)S(1)}, f32[32,24,4]{2,1,0:T(8,128)S(1)}, u32[]{:S(2)}, u32[]{:S(2)}) collective-permute-start(f32[32,24,4]{2,1,0:T(8,128)S(1)} %get-tuple-element.54), channel_id=1, source_target_pairs={{0,1},{1,0},{2,3},{3,2},{4,5},{5,4},{6,7},{7,6},{8,9},{9,8},{10,11... | collective-permute-start | bytes 36872 | tf_op jit(solution)/shard_map/ppermute | solution.py:16
  17.7 16.3 %collective-permute-start.7 = (f32[32,24,4]{2,1,0:T(8,128)S(1)}, f32[32,24,4]{2,1,0:T(8,128)S(1)}, u32[]{:S(2)}, u32[]{:S(2)}) collective-permute-start(f32[32,24,4]{2,1,0:T(8,128)S(1)} %get-tuple-element.55), channel_id=1, source_target_pairs={{1,0},{0,1},{3,2},{2,3},{5,4},{4,5},{7,6},{6,7},{9,8},{8,9},{11,10... | collective-permute-start | bytes 36872 | tf_op jit(solution)/shard_map/ppermute | solution.py:19
  40.1 7.6 %collective-permute-start.8 = (f32[32,4,256]{2,1,0:T(4,128)S(1)}, f32[32,4,256]{2,1,0:T(4,128)S(1)}, u32[]{:S(2)}, u32[]{:S(2)}) collective-permute-start(f32[32,4,256]{2,1,0:T(4,128)S(1)} %get-tuple-element.56), channel_id=1, source_target_pairs={{0,2},{2,4},{4,6},{6,8},{8,10},{10,12},{12,14},{14,0},{1,3},{3,5},... | collective-permute-start | bytes 393224 | tf_op jit(solution)/shard_map/ppermute | solution.py:16
  40.2 7.6 %collective-permute-start.9 = (f32[32,4,256]{2,1,0:T(4,128)S(1)}, f32[32,4,256]{2,1,0:T(4,128)S(1)}, u32[]{:S(2)}, u32[]{:S(2)}) collective-permute-start(f32[32,4,256]{2,1,0:T(4,128)S(1)} %get-tuple-element.57), channel_id=1, source_target_pairs={{2,0},{4,2},{6,4},{8,6},{10,8},{12,10},{14,12},{0,14},{3,1},{5,3},... | collective-permute-start | bytes 393224 | tf_op jit(solution)/shard_map/ppermute | solution.py:19
  43.9 6.3 %collective-permute-start.12 = (f32[32,4,256]{2,1,0:T(4,128)S(1)}, f32[32,4,256]{2,1,0:T(4,128)S(1)}, u32[]{:S(2)}, u32[]{:S(2)}) collective-permute-start(f32[32,4,256]{2,1,0:T(4,128)S(1)} %get-tuple-element.46), channel_id=1, source_target_pairs={{0,2},{2,4},{4,6},{6,8},{8,10},{10,12},{12,14},{14,0},{1,3},{3,5},... | collective-permute-start | bytes 393224 | tf_op jit(solution)/shard_map/ppermute | solution.py:16
  44.0 6.3 %collective-permute-start.13 = (f32[32,4,256]{2,1,0:T(4,128)S(1)}, f32[32,4,256]{2,1,0:T(4,128)S(1)}, u32[]{:S(2)}, u32[]{:S(2)}) collective-permute-start(f32[32,4,256]{2,1,0:T(4,128)S(1)} %get-tuple-element.47), channel_id=1, source_target_pairs={{2,0},{4,2},{6,4},{8,6},{10,8},{12,10},{14,12},{0,14},{3,1},{5,3},... | collective-permute-start | bytes 393224 | tf_op jit(solution)/shard_map/ppermute | solution.py:19
  48.1 12.1 %collective-permute-start.10 = (f32[32,24,4]{2,1,0:T(8,128)S(1)}, f32[32,24,4]{2,1,0:T(8,128)S(1)}, u32[]{:S(2)}, u32[]{:S(2)}) collective-permute-start(f32[32,24,4]{2,1,0:T(8,128)S(1)} %get-tuple-element.52), channel_id=1, source_target_pairs={{0,1},{1,0},{2,3},{3,2},{4,5},{5,4},{6,7},{7,6},{8,9},{9,8},{10,11... | collective-permute-start | bytes 36872 | tf_op jit(solution)/shard_map/ppermute | solution.py:16
  48.4 20.2 %collective-permute-start.11 = (f32[32,24,4]{2,1,0:T(8,128)S(1)}, f32[32,24,4]{2,1,0:T(8,128)S(1)}, u32[]{:S(2)}, u32[]{:S(2)}) collective-permute-start(f32[32,24,4]{2,1,0:T(8,128)S(1)} %get-tuple-element.53), channel_id=1, source_target_pairs={{1,0},{0,1},{3,2},{2,3},{5,4},{4,5},{7,6},{6,7},{9,8},{8,9},{11,10... | collective-permute-start | bytes 36872 | tf_op jit(solution)/shard_map/ppermute | solution.py:19
  50.6 26.4 %collective-permute-start.14 = (f32[32,24,4]{2,1,0:T(8,128)S(1)}, f32[32,24,4]{2,1,0:T(8,128)S(1)}, u32[]{:S(2)}, u32[]{:S(2)}) collective-permute-start(f32[32,24,4]{2,1,0:T(8,128)S(1)} %get-tuple-element.50), channel_id=1, source_target_pairs={{0,1},{1,0},{2,3},{3,2},{4,5},{5,4},{6,7},{7,6},{8,9},{9,8},{10,11... | collective-permute-start | bytes 36872 | tf_op jit(solution)/shard_map/ppermute | solution.py:16
  51.3 30.1 %collective-permute-start.15 = (f32[32,24,4]{2,1,0:T(8,128)S(1)}, f32[32,24,4]{2,1,0:T(8,128)S(1)}, u32[]{:S(2)}, u32[]{:S(2)}) collective-permute-start(f32[32,24,4]{2,1,0:T(8,128)S(1)} %get-tuple-element.51), channel_id=1, source_target_pairs={{1,0},{0,1},{3,2},{2,3},{5,4},{4,5},{7,6},{6,7},{9,8},{8,9},{11,10... | collective-permute-start | bytes 36872 | tf_op jit(solution)/shard_map/ppermute | solution.py:19
  88.1 1.7 copy-start.1
  88.1 1.7 copy-start.2
